TPU v7x, 64 devices: a 2x2x8 block of a 4x4x8 slice. The times are simulated.
64 devices in a mesh: dp: 4 (over x, y), ep: 16 (over z, core).
Axes of the slice: x: 2, y: 2, z: 8, core: 2. Of those that a mesh axis runs over, the one named last changes fastest.
The devices are a block of a 4x4x8 slice.
Arguments:
- hidden: bfloat16 [65536, 4096], P(('dp', 'ep')), parts along dimension 0
- ln_gamma: float32 [4096], replicated
- ln_beta: float32 [4096], replicated
- w_router: bfloat16 [4096, 16], replicated
- w_gate: bfloat16 [16, 4096, 448], P('ep')
- w_up: bfloat16 [16, 4096, 448], P('ep')
- w_down: bfloat16 [16, 448, 4096], P('ep')
- choice: int32 [65536, 2], P(('dp', 'ep')), parts along dimension 0
- mask_first: int32 [65536, 16], P(('dp', 'ep')), parts along dimension 0
- mask_second: int32 [65536, 16], P(('dp', 'ep')), parts along dimension 0
Outputs:
- output: bfloat16 [65536, 4096], P(('dp', 'ep')), parts along dimension 0
There are 4 independent parts. A program takes and returns all parts, laid end to end along the dimension named above; an argument that names none is the same for every part.
All inputs are finite; a program needn't handle non-finite values.
Results may differ from a plain program's by a relative error of at most 0.001.
Values are sent between devices in bfloat16 or wider.
A program may use at most 768 MiB of HBM per device.

v0:
```python
import jax
import jax.numpy as jnp
from jax import lax
from jax.sharding import PartitionSpec as P

LN_EPS = 1e-5


def layer_norm(token_rows, ln_gamma, ln_beta):
    values = token_rows.astype(jnp.float32)
    centred = values - jnp.mean(values, axis=-1, keepdims=True)
    variance = jnp.mean(centred * centred, axis=-1, keepdims=True)
    return (centred * lax.rsqrt(variance + LN_EPS) * ln_gamma + ln_beta).astype(jnp.bfloat16)


def sparse_gates(normed, w_router, choice, mask_first, mask_second):
    scores = jnp.dot(normed, w_router, preferred_element_type=jnp.float32)
    expert_ids = jnp.arange(w_router.shape[1], dtype=jnp.int32)
    mask_pair = jnp.stack([mask_first, mask_second], axis=1) > 0
    soft_probs = jax.nn.softmax(jnp.where(mask_pair, scores[:, None, :], -jnp.inf), axis=-1)
    return jnp.sum(jnp.where(choice[:, :, None] == expert_ids, soft_probs, 0.0), axis=-1)


def copy_slots(choice, experts, capacity):
    expert_ids = jnp.arange(experts, dtype=jnp.int32)
    hit_count = (choice[..., None] == expert_ids).astype(jnp.int32)
    per_token = jnp.sum(hit_count, axis=-2)
    before = jnp.cumsum(per_token, axis=-2) - per_token
    position = jnp.sum(hit_count * before[..., None, :], axis=-1)
    return position, position < capacity


def expert_mlp(expert_in, w_gate, w_up, w_down):
    gate_proj = jnp.einsum("secd,edf->secf", expert_in, w_gate, preferred_element_type=jnp.float32)
    up_proj = jnp.einsum("secd,edf->secf", expert_in, w_up, preferred_element_type=jnp.float32)
    inner_act = (jax.nn.silu(gate_proj) * up_proj).astype(jnp.bfloat16)
    return jnp.einsum("secf,efd->secd", inner_act, w_down, preferred_element_type=jnp.float32).astype(jnp.bfloat16)


def solution(mesh):
    group_size = mesh.shape["ep"]
    rows_spec = P(("dp", "ep"))

    def device_step(hidden, ln_gamma, ln_beta, w_router, w_gate, w_up, w_down, choice, mask_first, mask_second):
        tokens, row_width = hidden.shape
        local_experts = w_gate.shape[0]
        experts = local_experts * group_size
        capacity = (10 * tokens + 4 * experts - 1) // (4 * experts)
        slot_count = experts * capacity
        normed = layer_norm(hidden, ln_gamma, ln_beta)
        gate_vals = sparse_gates(normed, w_router, choice, mask_first, mask_second)
        position, kept_copy = copy_slots(choice, experts, capacity)
        flat_slot = jnp.where(kept_copy, choice * capacity + position, slot_count)
        token_ids = jnp.broadcast_to(jnp.arange(tokens, dtype=jnp.int32)[:, None], (tokens, 2))
        source_row = jnp.full((slot_count,), tokens, jnp.int32).at[flat_slot.reshape(-1)].set(token_ids.reshape(-1), mode="drop")
        send_rows = jnp.take(normed, source_row, axis=0, mode="fill", fill_value=0)
        recv_rows = lax.all_to_all(send_rows, "ep", 0, 0, tiled=True)
        expert_out = expert_mlp(recv_rows.reshape(group_size, local_experts, capacity, row_width), w_gate, w_up, w_down)
        back_rows = lax.all_to_all(expert_out.reshape(slot_count, row_width), "ep", 0, 0, tiled=True)
        picked = jnp.take(back_rows, flat_slot, axis=0, mode="fill", fill_value=0)
        mixed_out = hidden.astype(jnp.float32) + jnp.sum(gate_vals[:, :, None] * picked.astype(jnp.float32), axis=1)
        return mixed_out.astype(jnp.bfloat16)

    return jax.shard_map(device_step, mesh=mesh,
                         in_specs=(rows_spec, P(), P(), P(), P("ep"), P("ep"), P("ep"), rows_spec, rows_spec, rows_spec),
                         out_specs=rows_spec, check_vma=False)
```

profile of v0, /device:TPU:22, one launch (start us, length us, event | category | flops | bytes accessed | tf_op | source)
XLA Modules:
  0.0 1220.4 jit_solution(2954771826325718820)
XLA Ops:
  0.0 0.8 convert_reduce_fusion.1
  0.8 4.5 reduce-window.6
  5.7 0.7 select_reduce_fusion.1
  6.5 1.3 compare_and_fusion
  8.0 0.3 reshape.110
  8.4 0.3 reshape.136
  8.7 8.2 scatter_custom_fusion
  17.0 4.5 convert_reduce_fusion
  21.5 5.7 fusion.4
  27.3 9.2 fusion.7
  36.5 40.0 %gather_fusion = bf16[2560,4096]{1,0:T(8,128)(2,1)} fusion(bf16[1024,4096]{1,0:T(8,128)(2,1)} %fusion.7, s32[3072]{0:T(1024)S(1)} %pad_clamp_fusion), kind=kCustom, calls=%fused_computation | custom fusion | bytes 41953280 | tf_op jit(solution)/shard_map/jit(_take)/gather | solution.py:56
  76.5 10.3 broadcast_select_fusion.1
  86.8 464.3 %all_to_all.15 = bf16[16,160,4096]{2,1,0:T(8,128)(2,1)} all-to-all(bf16[16,160,4096]{2,1,0:T(8,128)(2,1)S(1)} %broadcast_select_fusion.1), channel_id=1, replica_groups=mesh['dp'=4,'ep'=16] {'ep'}, dimensions={0} | all-to-all | bytes 41943040 | tf_op jit(solution)/shard_map/all_to_all | solution.py:57
  551.0 16.8 %fusion.14 = f32[16,160,448]{2,1,0:T(8,128)} fusion(bf16[16,160,4096]{2,1,0:T(8,128)(2,1)} %all_to_all.15, bf16[1,4096,448]{1,2,0:T(8,128)(2,1)S(1)} %copy-done.7), kind=kOutput, calls=%fused_computation.27 | convolution fusion | flops 9395240960 | bytes 29229056 | tf_op jit(solution)/shard_map/secd,edf->secf/dot_general | solution.py:35
  567.8 30.5 %convolution_convert_fusion = bf16[16,160,4096]{2,1,0:T(8,128)(2,1)} fusion(bf16[1,448,4096]{2,1,0:T(8,128)(2,1)} %param.16, f32[16,160,448]{2,1,0:T(8,128)} %fusion.14, bf16[16,160,4096]{2,1,0:T(8,128)(2,1)} %all_to_all.15, bf16[1,4096,448]{1,2,0:T(8,128)(2,1)} %param.14), kind=kOutput, calls=%fused_computation.18 | convolution fusion | flops 18807848960 | bytes 53870592 | tf_op jit(solution)/shard_map/secf,efd->secd/dot_general | solution.py:37
  598.3 6.1 all-to-all-start.1
  604.4 0.3 copy.22
  605.0 0.3 reshape.126
  605.3 5.6 fusion.45
  611.3 467.6 %all-to-all-done.1 = bf16[16,160,4096]{2,1,0:T(8,128)(2,1)} async-done(((bf16[16,160,4096]{2,1,0:T(8,128)(2,1)}), bf16[16,160,4096]{2,1,0:T(8,128)(2,1)}, u32[]{:S(2)}, u32[]{:S(2)}) %all-to-all-start.1) | async-done | bytes 20971552 | tf_op jit(solution)/shard_map/all_to_all | solution.py:59
  1078.9 38.3 %gather_fusion.1 = bf16[2048,4096]{1,0:T(8,128)(2,1)} fusion(bf16[2560,4096]{1,0:T(8,128)(2,1)} %bitcast.22, s32[2048]{0:T(1024)S(1)} %broadcast_clamp_fusion), kind=kCustom, calls=%fused_computation.1 | custom fusion | bytes 33562624 | tf_op jit(solution)/shard_map/jit(_take)/gather | solution.py:60
  1117.2 27.0 %reshape.125 = bf16[1024,2,4096]{2,1,0:T(2,128)(2,1)} reshape(bf16[2048,4096]{1,0:T(8,128)(2,1)} %gather_fusion.1) | data formatting | bytes 33554432 | tf_op jit(solution)/shard_map/jit(_take)/gather | solution.py:60
  1144.2 64.2 %multiply_reduce_fusion = f32[1024,4096]{1,0:T(8,128)} fusion(bf16[1024,2,4096]{2,1,0:T(2,128)(2,1)} %reshape.125, pred[1024,2]{1,0:T(8,128)(4,1)S(1)} %copy.22, f32[1024,2]{1,0:T(8,128)S(1)} %copy.19), kind=kLoop, calls=%fused_computation.5 | loop fusion | flops 29360128 | bytes 33564672 | tf_op jit(solution)/shard_map/reduce_sum | solution.py:61
  1208.4 12.0 fusion.8
  (42 shorter events, 1.4 us)
Async XLA Ops:
  0.0 605.3 %copy-start = (bf16[4096,16]{0,1:T(8,128)(2,1)S(1)}, bf16[4096,16]{0,1:T(8,128)(2,1)}, u32[]{:S(2)}) copy-start(bf16[4096,16]{0,1:T(8,128)(2,1)} %param.13) | copy-start | bytes 393220
  0.0 27.3 %copy-start.5 = (f32[4096]{0:T(1024)S(1)}, f32[4096]{0:T(1024)}, u32[]{:S(2)}) copy-start(f32[4096]{0:T(1024)} %param.12) | copy-start | bytes 49156
  0.0 27.3 %copy-start.6 = (f32[4096]{0:T(1024)S(1)}, f32[4096]{0:T(1024)}, u32[]{:S(2)}) copy-start(f32[4096]{0:T(1024)} %param.11) | copy-start | bytes 49156
  7.8 28.7 %copy-start.1 = (s32[1024,2]{0,1:T(2,128)}, s32[1024,2]{0,1:T(2,128)S(1)}, u32[]{:S(2)}) copy-start(s32[1024,2]{0,1:T(2,128)S(1)} %get-tuple-element.6) | copy-start | bytes 24580
  86.8 464.3 %copy-start.7 = (bf16[1,4096,448]{1,2,0:T(8,128)(2,1)S(1)}, bf16[1,4096,448]{1,2,0:T(8,128)(2,1)}, u32[]{:S(2)}) copy-start(bf16[1,4096,448]{1,2,0:T(8,128)(2,1)} %param.15) | copy-start | bytes 11010052
  598.3 6.2 copy-start.4
  598.3 6.5 copy-start.2
  598.3 12.6 %copy-start.3 = (s32[1024,2]{0,1:T(2,128)S(1)}, s32[1024,2]{0,1:T(2,128)}, u32[]{:S(2)}) copy-start(s32[1024,2]{0,1:T(2,128)} %param.17) | copy-start | bytes 24580
  598.3 12.6 %copy-start.8 = (s32[1024,16]{0,1:T(8,128)S(1)}, s32[1024,16]{0,1:T(8,128)}, u32[]{:S(2)}) copy-start(s32[1024,16]{0,1:T(8,128)} %param.19) | copy-start | bytes 196612
  598.3 12.6 %copy-start.9 = (s32[1024,16]{0,1:T(8,128)S(1)}, s32[1024,16]{0,1:T(8,128)}, u32[]{:S(2)}) copy-start(s32[1024,16]{0,1:T(8,128)} %param.18) | copy-start | bytes 196612
  598.3 480.6 %all-to-all-start.1 = ((bf16[16,160,4096]{2,1,0:T(8,128)(2,1)}), bf16[16,160,4096]{2,1,0:T(8,128)(2,1)}, u32[]{:S(2)}, u32[]{:S(2)}) async-start(bf16[16,160,4096]{2,1,0:T(8,128)(2,1)} %convolution_convert_fusion), calls=%async_computation.1 | async-start | bytes 41943040 | tf_op jit(solution)/shard_map/all_to_all | solution.py:59
where the time goes:
time: 1220 us
  waiting for transfers between devices  468 us (38%)
  blocking collectives  464 us (38%)
  local copies, waits for them, and re-layouts  116 us (10%)
  other arithmetic  114 us (9%)
  matrix products  52.9 us (4%)
    all_to_all x1, waiting for transfers between devices, device_step(): lax.all_to_all(expert_out.reshape(slot_count, row_width), 'ep', 0, 0, til...  468 us
    all_to_all x1, blocking collectives, device_step(): recv_rows = lax.all_to_all(send_rows, 'ep', 0, 0, tiled=True)  464 us
    gather x2, local copies, waits for them, and re-layouts, device_step(): picked = jnp.take(back_rows, flat_slot, axis=0, mode='fill', fill_value=0)  65.3 us
    reduce_sum x1, other arithmetic, device_step(): jnp.sum(gate_vals[:, :, None] * picked.astype(jnp.float32), axis=1)  64.2 us
    gather x1, local copies, waits for them, and re-layouts, device_step(): send_rows = jnp.take(normed, source_row, axis=0, mode='fill', fill_value=0)  40 us
    dot_general x1, matrix products, expert_mlp(): jnp.einsum('secf,efd->secd', inner_act, w_down, preferred_element_type=jn...  30.5 us
  transfers between devices with their start and end apart: 1, of which 1 were waited for; matrix products, arithmetic and copies ran while one was open for 1% of the time, Pallas kernels for 0%

commit v1 on v0

v1 whole, which is shorter than its diff:
```python
import functools
import math

import jax
import jax.numpy as jnp
from jax import lax
from jax.experimental import pallas as pl
from jax.experimental.pallas import tpu as pltpu
from jax.sharding import PartitionSpec as P

LN_EPS = 1e-5
LANES = 128
PARTS = 16
DEPTH = 4
MESH = pl.DeviceIdType.MESH


def moe_kernel(sizes, hidden_ref, gamma_ref, beta_ref, router_ref, gu_ref, wd_ref, choice_ref, first_ref, second_ref,
               out_ref, gu_all, wd_all,
               normed, total, gu_buf, wd_buf, row_buf, inner_buf, gate_table, gate_wide,
               ring_send, ring_recv, side_send, side_recv, pair_send, pair_recv, own_send, own_recv,
               row_sem, load_sem):
    ring, columns, capacity = sizes
    tokens, width = hidden_ref.shape
    ff = wd_ref.shape[0]
    experts = gu_all.shape[0]
    half = tokens // 2
    tile = tokens // 8
    part_rows = width // PARTS
    rounds = 4 * (ring - 1)
    dp = lax.axis_index("dp")
    ep = lax.axis_index("ep")
    z, core = ep // 2, ep % 2
    x, y = dp // columns, dp % columns
    parity = (x + y) % 2
    after, before = ((z + 1) % ring) * 2 + core, ((z + ring - 1) % ring) * 2 + core
    partner = z * 2 + 1 - core
    x_peer = (x + 1 - 2 * (x % 2)) * columns + y
    y_peer = x * columns + y + 1 - 2 * (y % 2)
    places = ((dp, after), (dp, before), (x_peer, ep), (y_peer, ep), (dp, partner))

    barrier = pltpu.get_barrier_semaphore()
    for place in places:
        pl.semaphore_signal(barrier, inc=1, device_id=place, device_id_type=MESH)
    pl.semaphore_wait(barrier, len(places))

    def pieces(gu_source, wd_source, expert, part):
        rows = pl.ds(pl.multiple_of(part * part_rows, part_rows), part_rows)
        gu_to, wd_to = gu_all.at[expert, rows, :], wd_all.at[expert, :, rows]
        if gu_source is None:
            return (gu_to, gu_to), (wd_to, wd_to)
        return (gu_source.at[rows, :], gu_to), (wd_source.at[:, rows], wd_to)

    def copies(both, send, recv, place):
        return [pltpu.make_async_remote_copy(src_ref=src, dst_ref=dst, send_sem=send.at[kind], recv_sem=recv.at[kind],
                                             device_id=place, device_id_type=MESH)
                for kind, (src, dst) in enumerate(both)]

    def ring_part(flow, index):
        return (index + 4 * flow) % 8

    def ring_copy(flow, index, own):
        expert = ((z + (index // 8) * (2 * flow - 1) + ring) % ring) * 2 + core
        part = 8 * parity + ring_part(flow, index)
        both = pieces(gu_ref if own else None, wd_ref if own else None, expert, part)
        return copies(both, ring_send.at[flow, index], ring_recv.at[flow, index], places[flow])

    def came(flow, index, of_core, of_parity):
        expert = ((z + (1 + index // 8) * (2 * flow - 1) + ring) % ring) * 2 + of_core
        return pieces(None, None, expert, 8 * of_parity + ring_part(flow, index))

    def ring_arrival(flow, index):
        return copies(came(flow, index, core, parity), ring_send.at[flow, index], ring_recv.at[flow, index], places[flow])

    def side_copy(flow, index, of_parity):
        carried = (index // 4 + flow) % 2
        return copies(came(carried, index, core, of_parity), side_send.at[flow, index], side_recv.at[flow, index],
                      places[2 + flow])

    def pair_copy(flow, index, of_core):
        if flow < 2:
            both = came(flow, index, of_core, parity)
        else:
            both = came((index // 4 + flow) % 2, index, of_core, 1 - parity)
        return copies(both, pair_send.at[flow, index], pair_recv.at[flow, index], places[4])

    def own_copy(expert):
        return copies(((gu_ref, gu_all.at[expert]), (wd_ref, wd_all.at[expert])), own_send, own_recv, places[4])

    def start(group):
        for copy in group:
            copy.start()

    def wait_recv(group):
        for copy in group:
            copy.wait_recv()

    def wait_send(group):
        for copy in group:
            copy.wait_send()

    def row_load(index):
        rows = pl.ds(pl.multiple_of(index * tile, tile), tile)
        return pltpu.make_async_copy(hidden_ref.at[rows, :], row_buf.at[index % 4], row_sem.at[index % 4])

    def expert_of(turn):
        place = (turn + 2) % 4
        return ((z + ((turn + 2) // 4) * (2 * (place // 2) - 1) + ring) % ring) * 2 + core + (place % 2) * (1 - 2 * core)

    def loads(gu_source, wd_source, slot):
        return (pltpu.make_async_copy(gu_source, gu_buf.at[slot], load_sem.at[slot, 0]),
                pltpu.make_async_copy(wd_source, wd_buf.at[slot, pl.ds(0, ff), :], load_sem.at[slot, 1]))

    def expert_loads(turn):
        expert = expert_of(turn)
        return loads(gu_all.at[expert], wd_all.at[expert], turn % 2)

    start(loads(gu_ref, wd_ref, 0))
    for index in range(4):
        row_load(index).start()
    for index in range(DEPTH):
        for flow in range(2):
            start(ring_copy(flow, index, True))
    start(own_copy(ep))
    padded = wd_buf.shape[1]
    wd_buf[:, pl.ds(ff, padded - ff), :] = jnp.zeros((2, padded - ff, width), wd_buf.dtype)

    def norm_tile(index):
        row_load(index).wait()
        rows = pl.ds(pl.multiple_of(index * tile, tile), tile)
        values = row_buf[index % 4].astype(jnp.float32)
        total[rows, :] = values
        centred = values - jnp.mean(values, axis=-1, keepdims=True)
        variance = jnp.mean(centred * centred, axis=-1, keepdims=True)
        normed[rows, :] = (centred * lax.rsqrt(variance + LN_EPS) * gamma_ref[...] + beta_ref[...]).astype(jnp.bfloat16)

        @pl.when(index + 4 < 8)
        def _():
            row_load(index + 4).start()

    def hits(rows, pick, count):
        ids = lax.broadcasted_iota(jnp.int32, (count, experts), 1)
        return ids == choice_ref[rows, pl.ds(pick, 1)]

    def gate_tile(index):
        step = 2 * tile
        rows = pl.ds(pl.multiple_of(index * step, step), step)
        scores = jnp.dot(normed[rows, :], router_ref[...], preferred_element_type=jnp.float32)
        every = pl.ds(0, tokens)
        per_token = sum(jnp.where(hits(every, pick, tokens), 1.0, 0.0) for pick in range(2)).astype(jnp.bfloat16)
        earlier = (lax.broadcasted_iota(jnp.int32, (step, tokens), 1)
                   < lax.broadcasted_iota(jnp.int32, (step, tokens), 0) + index * step)
        position = jnp.dot(jnp.where(earlier, 1.0, 0.0).astype(jnp.bfloat16), per_token, preferred_element_type=jnp.float32)
        table = jnp.full((step, experts), -1.0, jnp.float32)
        for pick, mask_ref in enumerate((first_ref, second_ref)):
            hit = hits(rows, pick, step)
            masked = jnp.where(mask_ref[rows, :] > 0, scores, -jnp.inf)
            powers = jnp.exp(masked - jnp.max(masked, axis=-1, keepdims=True))
            probs = powers / jnp.sum(powers, axis=-1, keepdims=True)
            table = jnp.where(hit & (position < capacity), probs, table)
        gate_table[rows, :] = table

    def expert_unit(unit):
        turn, part = unit // 2, unit % 2
        slot = turn % 2
        expert = expert_of(turn)

        @pl.when(part == 0)
        def _():
            for copy in expert_loads(turn):
                copy.wait()

        @pl.when((part == 1) & (turn == 0))
        def _():
            wait_recv(own_copy(partner))

        @pl.when((part == 1) & (turn + 1 < experts))
        def _():
            start(expert_loads(turn + 1))

        rows = pl.ds(pl.multiple_of(part * half, half), half)
        ids = lax.broadcasted_iota(jnp.int32, (half, experts), 1)
        gates = jnp.sum(jnp.where(ids == expert, gate_table[rows, :], 0.0), axis=-1, keepdims=True)
        gate_wide[...] = jnp.broadcast_to(gates, gate_wide.shape)

        def inner_tile(index, _):
            lanes = pl.ds(pl.multiple_of(index * 2 * LANES, 2 * LANES), 2 * LANES)
            both = jnp.dot(normed[rows, :], gu_buf[slot, :, lanes], preferred_element_type=jnp.float32)
            value = jax.nn.silu(both[:, :LANES]) * both[:, LANES:]
            inner_buf[:, pl.ds(pl.multiple_of(index * LANES, LANES), LANES)] = value.astype(jnp.bfloat16)
            return 0

        full = ff // LANES
        lax.fori_loop(0, full, inner_tile, 0)
        rest = ff - full * LANES
        both = jnp.dot(normed[rows, :], gu_buf[slot, :, pl.ds(full * 2 * LANES, LANES)], preferred_element_type=jnp.float32)
        value = jax.nn.silu(both) * pltpu.roll(both, LANES - rest, 1)
        lane = lax.broadcasted_iota(jnp.int32, value.shape, 1)
        inner_buf[:, pl.ds(full * LANES, LANES)] = jnp.where(lane < rest, value, 0.0).astype(jnp.bfloat16)

        step = width // PARTS

        def out_tile(index, _):
            lanes = pl.ds(pl.multiple_of(index * step, step), step)
            made = jnp.dot(inner_buf[...], wd_buf[slot, :, lanes], preferred_element_type=jnp.float32)
            made = made.astype(jnp.bfloat16).astype(jnp.float32)
            gate = jnp.concatenate([gate_wide[...]] * (step // LANES), axis=1) if step > LANES else gate_wide[:, :step]
            total[rows, lanes] += jnp.where(gate >= 0.0, gate * made, 0.0)
            return 0

        lax.fori_loop(0, PARTS, out_tile, 0)

    first_double = 4 * ring - 7

    def begin(step):
        return jnp.maximum(step - 5, 0) + jnp.maximum(step - first_double, 0)

    def step_body(step, _):
        @pl.when(step < rounds)
        def _():
            for flow in range(2):
                wait_recv(ring_arrival(flow, step))
            ahead = step + DEPTH
            for flow in range(2):
                @pl.when(ahead < 8)
                def _():
                    start(ring_copy(flow, ahead, True))

                @pl.when((ahead >= 8) & (ahead < rounds))
                def _():
                    start(ring_copy(flow, ahead, False))
            for flow in range(2):
                start(side_copy(flow, step, parity))
            for flow in range(2):
                start(pair_copy(flow, step, core))

        @pl.when((step >= 1) & (step <= rounds))
        def _():
            for flow in range(2):
                wait_recv(side_copy(flow, step - 1, 1 - parity))
            for flow in range(2):
                start(pair_copy(2 + flow, step - 1, core))

        @pl.when(step >= 2)
        def _():
            for flow in range(4):
                wait_recv(pair_copy(flow, step - 2, 1 - core))

        @pl.when(step < 4)
        def _():
            norm_tile(2 * step)
            norm_tile(2 * step + 1)

        @pl.when(step == 4)
        def _():
            lax.fori_loop(0, 4, lambda index, _: (gate_tile(index), 0)[1], 0)

        low = begin(step)
        high = jnp.where(step == rounds + 1, 2 * experts, begin(step + 1))
        lax.fori_loop(low, high, lambda unit, _: (expert_unit(unit), 0)[1], 0)
        return 0

    lax.fori_loop(0, rounds + 2, step_body, 0)

    def row_store(index):
        rows = pl.ds(pl.multiple_of(index * tile, tile), tile)
        return pltpu.make_async_copy(row_buf.at[index % 4], out_ref.at[rows, :], row_sem.at[index % 4])

    def store_tile(index, _):
        @pl.when(index >= 4)
        def _():
            row_store(index - 4).wait()
        rows = pl.ds(pl.multiple_of(index * tile, tile), tile)
        row_buf[index % 4] = total[rows, :].astype(row_buf.dtype)
        row_store(index).start()
        return 0

    lax.fori_loop(0, 8, store_tile, 0)
    for index in range(4, 8):
        row_store(index).wait()

    def finish(index, _):
        for flow in range(2):
            wait_send(ring_copy(flow, index, False))
            wait_send(side_copy(flow, index, parity))
        for flow in range(4):
            wait_send(pair_copy(flow, index, core))
        return 0

    lax.fori_loop(0, rounds, finish, 0)
    wait_send(own_copy(ep))


def pack_gate_up(w_gate, w_up):
    ff = w_gate.shape[1]
    full = ff // LANES
    pieces = []
    for index in range(full + 1):
        low, high = index * LANES, min(ff, (index + 1) * LANES)
        pieces += [w_gate[:, low:high], w_up[:, low:high]]
    return jnp.concatenate(pieces, axis=1)


def solution(mesh):
    group_size = mesh.shape["ep"]
    columns = math.isqrt(mesh.shape["dp"])
    rows_spec = P(("dp", "ep"))

    def device_step(hidden, ln_gamma, ln_beta, w_router, w_gate, w_up, w_down, choice, mask_first, mask_second):
        tokens, width = hidden.shape
        experts = w_gate.shape[0] * group_size
        ff = w_gate.shape[2]
        capacity = (10 * tokens + 4 * experts - 1) // (4 * experts)
        ring = group_size // 2
        rounds = 4 * (ring - 1)
        padded = -(-ff // LANES) * LANES
        packed = pack_gate_up(w_gate[0], w_up[0])
        dma = pltpu.SemaphoreType.DMA
        whole = pl.BlockSpec(memory_space=pl.ANY)
        local = pl.BlockSpec(memory_space=pltpu.VMEM)
        out, _, _ = pl.pallas_call(
            functools.partial(moe_kernel, (ring, columns, capacity)),
            out_shape=(jax.ShapeDtypeStruct(hidden.shape, hidden.dtype),
                       jax.ShapeDtypeStruct((experts, width, 2 * ff), w_gate.dtype),
                       jax.ShapeDtypeStruct((experts, ff, width), w_down.dtype)),
            in_specs=[whole, local, local, local, whole, whole, local, local, local],
            out_specs=(whole, whole, whole),
            scratch_shapes=[
                pltpu.VMEM((tokens, width), jnp.bfloat16),
                pltpu.VMEM((tokens, width), jnp.float32),
                pltpu.VMEM((2, width, 2 * ff), w_gate.dtype),
                pltpu.VMEM((2, padded, width), w_down.dtype),
                pltpu.VMEM((4, tokens // 8, width), hidden.dtype),
                pltpu.VMEM((tokens // 2, padded), jnp.bfloat16),
                pltpu.VMEM((tokens, experts), jnp.float32),
                pltpu.VMEM((tokens // 2, LANES), jnp.float32),
                dma((2, rounds, 2)), dma((2, rounds, 2)),
                dma((2, rounds, 2)), dma((2, rounds, 2)),
                dma((4, rounds, 2)), dma((4, rounds, 2)),
                dma((2,)), dma((2,)),
                dma((4,)), dma((2, 2)),
            ],
            compiler_params=pltpu.CompilerParams(collective_id=0, has_side_effects=True, vmem_limit_bytes=67043328),
            name="moe",
        )(hidden, ln_gamma.reshape(1, width), ln_beta.reshape(1, width), w_router, packed, w_down[0],
          choice, mask_first, mask_second)
        return out

    return jax.shard_map(device_step, mesh=mesh,
                         in_specs=(rows_spec, P(), P(), P(), P("ep"), P("ep"), P("ep"), rows_spec, rows_spec, rows_spec),
                         out_specs=rows_spec, check_vma=False)
```

time: 1220 us -> 584 us (0.48)
  Pallas kernels: 0 us -> 533 us
  waiting for transfers between devices: 468 us -> 0 us
  blocking collectives: 464 us -> 0 us
  other arithmetic: 114 us -> 0 us
  local copies, waits for them, and re-layouts: 116 us -> 49 us
  matrix products: 52.9 us -> 0 us
    pallas_call x0 -> x1, Pallas kernels: none -> 533 us  [device_step(): pl.pallas_call(functools.partial(moe_kernel, (ring, columns, capacity)),...]
    all_to_all x1 -> x0, waiting for transfers between devices: 468 us -> none  [device_step(): lax.all_to_all(expert_out.reshape(slot_count, row_width), 'ep', 0, 0, til...]
    all_to_all x1 -> x0, blocking collectives: 464 us -> none  [device_step(): recv_rows = lax.all_to_all(send_rows, 'ep', 0, 0, tiled=True)]
    gather x3 -> x0, local copies, waits for them, and re-layouts: 105 us -> none  [the longest x2 65.3 us: device_step(): picked = jnp.take(back_rows, flat_slot, axis=0, mode='fill', fill_value=0)]
    reduce_sum x5 -> x0, other arithmetic: 76 us -> none  [the longest x1 64.2 us: device_step(): jnp.sum(gate_vals[:, :, None] * picked.astype(jnp.float32), axis=1)]
    dot_general x3 -> x0, matrix products: 52.9 us -> none  [the longest x1 30.5 us: expert_mlp(): jnp.einsum('secf,efd->secd', inner_act, w_down, preferred_element_type=jn...]
    unnamed x21 -> x7, local copies, waits for them, and re-layouts: 0.06 us -> 28.3 us
    convert_element_type x2 -> x0, other arithmetic: 21.2 us -> none  [the longest x1 12 us: device_step(): return mixed_out.astype(jnp.bfloat16)]
  transfers between devices with their start and end apart: 1 -> 0, of which waited for: 1 -> 0; matrix products, arithmetic and copies ran while one was open for 1% -> 0% of each run, Pallas kernels for 0% -> 0%
where the time goes in v1:
time: 584 us; the launch traced here: 582 us
  Pallas kernels  533 us (91%)
  local copies, waits for them, and re-layouts  49 us (8%)
    pallas_call x1, Pallas kernels, device_step(): pl.pallas_call(functools.partial(moe_kernel, (ring, columns, capacity)),...  533 us
    unnamed x7, local copies, waits for them, and re-layouts  28.3 us

profile of v1, /device:TPU:22, one launch (start us, length us, event | category | flops | bytes accessed | tf_op | source)
XLA Modules:
  0.0 582.4 jit_solution(1184379327151143720)
XLA Ops:
  0.0 1.7 copy.14.choice_ref
  1.7 1.8 copy.15.first_ref
  3.5 1.9 copy.16.second_ref
  5.4 2.2 copy.13.router_ref
  7.6 6.4 %copy.11 = bf16[1,4096,448]{2,1,0:T(8,128)(2,1)} copy(bf16[1,4096,448]{1,2,0:T(8,128)(2,1)} %param.14) | data formatting | bytes 7340032 | tf_op args[4]
  14.0 2.3 slice.38
  16.3 6.3 %copy.12 = bf16[1,4096,448]{2,1,0:T(8,128)(2,1)} copy(bf16[1,4096,448]{1,2,0:T(8,128)(2,1)} %param.15) | data formatting | bytes 7340032 | tf_op args[5]
  22.7 2.3 slice.39
  25.0 4.7 fusion
  29.7 11.4 %concatenate.3.gu_ref = bf16[4096,896]{1,0:T(8,128)(2,1)} concatenate(bf16[4096,128]{1,0:T(8,128)(2,1)} %get-tuple-element.13, bf16[4096,128]{1,0:T(8,128)(2,1)S(1)} %get-tuple-element.9, bf16[4096,128]{1,0:T(8,128)(2,1)} %get-tuple-element.14, bf16[4096,128]{1,0:T(8,128)(2,1)S(1)} %get-tuple-element.8, bf16[4096,128]{1,0:T(8,128)(2,1)} %get-tuple-element.15, ...), dimensions={1} | concatenate | bytes 14680064 | tf_op jit(solution)/shard_map/concatenate | solution.py:301
  41.1 533.4 %moe.1 = (bf16[1024,4096]{1,0:T(8,128)(2,1)}, bf16[16,4096,896]{2,1,0:T(8,128)(2,1)}, bf16[16,448,4096]{2,1,0:T(8,128)(2,1)}) custom-call(bf16[1024,4096]{1,0:T(8,128)(2,1)} %hidden_ref.1, f32[1,4096]{1,0:T(1,128)} %bitcast.10, f32[1,4096]{1,0:T(1,128)} %bitcast.11, bf16[4096,16]{1,0:T(8,128)(2,1)} %copy.13.router_ref, bf16[4096,896]{1,0:T(8,128)(2,1)} %concatenate.3.gu_ref, ...), custom_call_target="tpu_custom_call" | custom-call | tf_op jit(solution)/shard_map/moe/pallas_call | solution.py:321
  574.6 7.9 %copy.18 = bf16[1024,4096]{1,0:T(8,128)(2,1)} copy(bf16[1024,4096]{1,0:T(8,128)(2,1)} %get-tuple-element.6) | data formatting | bytes 16777216

commit v2 on v1

v2 whole, which is shorter than its diff:
```python
import functools
import math

import jax
import jax.numpy as jnp
from jax import lax
from jax.experimental import pallas as pl
from jax.experimental.pallas import tpu as pltpu
from jax.sharding import PartitionSpec as P

LN_EPS = 1e-5
LANES = 128
SPLIT = 2
DEPTH = 3
MESH = pl.DeviceIdType.MESH


def quotient(value, by):
    return lax.div(value, jnp.int32(by))


def remainder(value, by):
    return lax.rem(value, jnp.int32(by))


def moe_kernel(sizes, hidden_ref, gamma_ref, beta_ref, router_ref, own_ref, choice_ref, first_ref, second_ref,
               out_ref, gathered,
               normed, total, gu_buf, wd_buf, row_buf, inner_buf, gate_table, gate_wide,
               ring_send, ring_recv, side_send, side_recv, pair_send, pair_recv, own_send, own_recv,
               row_sem, load_sem):
    ring, columns, capacity = sizes
    tokens, width = hidden_ref.shape
    ff = own_ref.shape[1]
    experts = gathered.shape[0]
    half = tokens // 2
    tile = tokens // 8
    turns = 2 * SPLIT
    part_rows = ff // (2 * turns)
    rounds = SPLIT * (ring - 1)
    dp = lax.axis_index("dp")
    ep = lax.axis_index("ep")
    z, core = quotient(ep, 2), remainder(ep, 2)
    x, y = quotient(dp, columns), remainder(dp, columns)
    parity = remainder(x + y, 2)
    after, before = remainder(z + 1, ring) * 2 + core, remainder(z + ring - 1, ring) * 2 + core
    partner = z * 2 + 1 - core
    x_peer = (x + 1 - 2 * remainder(x, 2)) * columns + y
    y_peer = x * columns + y + 1 - 2 * remainder(y, 2)
    places = ((dp, after), (dp, before), (x_peer, ep), (y_peer, ep), (dp, partner))

    barrier = pltpu.get_barrier_semaphore()
    for place in places:
        pl.semaphore_signal(barrier, inc=1, device_id=place, device_id_type=MESH)
    pl.semaphore_wait(barrier, len(places))

    def piece(expert, part, own=False):
        rows = pl.ds(pl.multiple_of(part * part_rows, 8), part_rows)
        target = gathered.at[expert, :, rows, :]
        return (own_ref.at[:, rows, :] if own else target), target

    def copies(both, send, recv, place):
        return [pltpu.make_async_remote_copy(src_ref=both[0], dst_ref=both[1], send_sem=send, recv_sem=recv,
                                             device_id=place, device_id_type=MESH)]

    def ring_part(flow, index):
        return remainder(index + SPLIT * flow, turns)

    def far(flow, hops):
        return remainder(z + hops * (2 * flow - 1) + ring, ring) * 2

    def ring_copy(flow, index, own):
        both = piece(far(flow, quotient(index, turns)) + core, turns * parity + ring_part(flow, index), own)
        return copies(both, ring_send.at[flow, index], ring_recv.at[flow, index], places[flow])

    def came(flow, index, of_core, of_parity):
        return piece(far(flow, 1 + quotient(index, turns)) + of_core, turns * of_parity + ring_part(flow, index))

    def ring_arrival(flow, index):
        return copies(came(flow, index, core, parity), ring_send.at[flow, index], ring_recv.at[flow, index], places[flow])

    def carried(flow, index):
        return remainder(quotient(index, SPLIT) + flow, 2)

    def side_copy(flow, index, of_parity):
        return copies(came(carried(flow, index), index, core, of_parity), side_send.at[flow, index],
                      side_recv.at[flow, index], places[2 + flow])

    def pair_copy(flow, index, of_core):
        if flow < 2:
            both = came(flow, index, of_core, parity)
        else:
            both = came(carried(flow, index), index, of_core, 1 - parity)
        return copies(both, pair_send.at[flow, index], pair_recv.at[flow, index], places[4])

    def own_copy(expert):
        return copies((own_ref, gathered.at[expert]), own_send.at[0], own_recv.at[0], places[4])

    def start(group):
        for copy in group:
            copy.start()

    def wait_recv(group):
        for copy in group:
            copy.wait_recv()

    def wait_send(group):
        for copy in group:
            copy.wait_send()

    def row_load(index):
        rows = pl.ds(pl.multiple_of(index * tile, tile), tile)
        slot = remainder(index, 4)
        return pltpu.make_async_copy(hidden_ref.at[rows, :], row_buf.at[slot], row_sem.at[slot])

    def expert_of(turn):
        high, low = quotient(remainder(turn + 2, 4), 2), remainder(turn, 2)
        edge = (turn < 2) | (turn >= experts - 2)
        kind = jnp.where(edge, low, high)
        return far(jnp.where(edge, high, low), quotient(turn + 2, 4)) + core + kind * (1 - 2 * core)

    full, rest = ff // LANES, ff % LANES

    def loads(source, slot):
        made = [pltpu.make_async_copy(source.at[2], wd_buf.at[slot, pl.ds(0, ff), :], load_sem.at[slot, 0])]
        for index in range(full + 1):
            count = LANES if index < full else rest
            for kind in range(2):
                made.append(pltpu.make_async_copy(
                    source.at[kind, pl.ds(index * LANES, count), :],
                    gu_buf.at[slot, pl.ds(index * 2 * LANES + kind * count, count), :],
                    load_sem.at[slot, 1 + 2 * index + kind]))
        return made

    def expert_loads(turn):
        return loads(gathered.at[expert_of(turn)], remainder(turn, 2))

    start(loads(own_ref, 0))
    for index in range(4):
        row_load(index).start()
    for index in range(DEPTH):
        for flow in range(2):
            start(ring_copy(flow, index, True))
    start(own_copy(ep))
    padded = wd_buf.shape[1]
    wd_buf[:, pl.ds(ff, padded - ff), :] = jnp.zeros((2, padded - ff, width), wd_buf.dtype)

    def norm_tile(index):
        row_load(index).wait()
        rows = pl.ds(pl.multiple_of(index * tile, tile), tile)
        values = row_buf[remainder(index, 4)].astype(jnp.float32)
        total[rows, :] = values
        centred = values - jnp.mean(values, axis=-1, keepdims=True)
        variance = jnp.mean(centred * centred, axis=-1, keepdims=True)
        normed[rows, :] = (centred * lax.rsqrt(variance + LN_EPS) * gamma_ref[...] + beta_ref[...]).astype(jnp.bfloat16)

        @pl.when(index + 4 < 8)
        def _():
            row_load(index + 4).start()

    def hits(rows, pick, count):
        ids = lax.broadcasted_iota(jnp.int32, (experts, count), 0)
        return ids == choice_ref[pl.ds(pick, 1), rows]

    def gate_tile(index):
        step = 2 * tile
        rows = pl.ds(pl.multiple_of(index * step, step), step)
        scores = lax.dot_general(normed[rows, :], router_ref[...], (((1,), (1,)), ((), ())),
                                 preferred_element_type=jnp.float32)
        every = pl.ds(0, tokens)
        per_token = sum(jnp.where(hits(every, pick, tokens), 1.0, 0.0) for pick in range(2)).astype(jnp.bfloat16)
        earlier = (lax.broadcasted_iota(jnp.int32, (step, tokens), 1)
                   < lax.broadcasted_iota(jnp.int32, (step, tokens), 0) + index * step)
        position = lax.dot_general(jnp.where(earlier, 1.0, 0.0).astype(jnp.bfloat16), per_token, (((1,), (1,)), ((), ())),
                                   preferred_element_type=jnp.float32)
        table = jnp.full((step, experts), -1.0, jnp.float32)
        for pick, mask_ref in enumerate((first_ref, second_ref)):
            hit = jnp.where(hits(rows, pick, step), 1.0, 0.0).T > 0.0
            masked = jnp.where(mask_ref[:, rows].T > 0, scores, -jnp.inf)
            powers = jnp.exp(masked - jnp.max(masked, axis=-1, keepdims=True))
            probs = powers / jnp.sum(powers, axis=-1, keepdims=True)
            table = jnp.where(hit & (position < capacity), probs, table)
        gate_table[rows, :] = table

    def expert_unit(unit):
        turn, part = quotient(unit, 2), remainder(unit, 2)
        slot = remainder(turn, 2)
        expert = expert_of(turn)

        @pl.when(part == 0)
        def _():
            for copy in expert_loads(turn):
                copy.wait()

        @pl.when((part == 1) & (turn == 0))
        def _():
            wait_recv(own_copy(partner))

        @pl.when((part == 1) & (turn + 1 < experts))
        def _():
            start(expert_loads(turn + 1))

        rows = pl.ds(pl.multiple_of(part * half, half), half)
        ids = lax.broadcasted_iota(jnp.int32, (half, experts), 1)
        gates = jnp.sum(jnp.where(ids == expert, gate_table[rows, :], 0.0), axis=-1, keepdims=True)
        gate_wide[...] = jnp.broadcast_to(gates, gate_wide.shape)

        def project(outs):
            return lax.dot_general(normed[rows, :], gu_buf[slot, outs, :], (((1,), (1,)), ((), ())),
                                   preferred_element_type=jnp.float32)

        def inner_tile(index, _):
            both = project(pl.ds(pl.multiple_of(index * 2 * LANES, 2 * LANES), 2 * LANES))
            value = jax.nn.silu(both[:, :LANES]) * both[:, LANES:]
            inner_buf[:, pl.ds(pl.multiple_of(index * LANES, LANES), LANES)] = value.astype(jnp.bfloat16)
            return 0

        lax.fori_loop(0, full, inner_tile, 0)
        both = project(pl.ds(full * 2 * LANES, 2 * rest))
        value = jax.nn.silu(both) * pltpu.roll(both, LANES - rest, 1)
        lane = lax.broadcasted_iota(jnp.int32, value.shape, 1)
        inner_buf[:, pl.ds(full * LANES, LANES)] = jnp.where(lane < rest, value, 0.0).astype(jnp.bfloat16)

        step = min(width, 2 * LANES)

        def out_tile(index, _):
            lanes = pl.ds(pl.multiple_of(index * step, step), step)
            made = jnp.dot(inner_buf[...], wd_buf[slot, :, lanes], preferred_element_type=jnp.float32)
            made = made.astype(jnp.bfloat16).astype(jnp.float32)
            gate = jnp.concatenate([gate_wide[...]] * (step // LANES), axis=1) if step > LANES else gate_wide[:, :step]
            total[rows, lanes] += jnp.where(gate >= 0.0, gate * made, 0.0)
            return 0

        lax.fori_loop(0, width // step, out_tile, 0)

    last = rounds - 2

    def begin(step):
        late = jnp.where(step == last, 2 * experts - 13, jnp.where(step == last + 1, 2 * experts - 9, 2 * experts - 5))
        late = jnp.where(step < last + 3, late, jnp.where(step == last + 3, 2 * experts - 4, 2 * experts))
        return jnp.where(step < last, 2 * jnp.maximum(step - 3, 0), late)

    def step_body(step, _):
        @pl.when(step < rounds)
        def _():
            for flow in range(2):
                wait_recv(ring_arrival(flow, step))
            ahead = step + DEPTH
            for flow in range(2):
                @pl.when(ahead < turns)
                def _():
                    start(ring_copy(flow, ahead, True))

                @pl.when((ahead >= turns) & (ahead < rounds))
                def _():
                    start(ring_copy(flow, ahead, False))
            for flow in range(2):
                start(side_copy(flow, step, parity))
            for flow in range(2):
                start(pair_copy(flow, step, core))

        @pl.when((step >= 1) & (step <= rounds))
        def _():
            for flow in range(2):
                wait_recv(side_copy(flow, step - 1, 1 - parity))
            for flow in range(2):
                start(pair_copy(2 + flow, step - 1, core))

        @pl.when(step >= 2)
        def _():
            for flow in range(4):
                wait_recv(pair_copy(flow, step - 2, 1 - core))

        @pl.when(step < 2)
        def _():
            lax.fori_loop(4 * step, 4 * step + 4, lambda index, _: (norm_tile(index), 0)[1], 0)

        @pl.when(step == 1)
        def _():
            lax.fori_loop(0, 4, lambda index, _: (gate_tile(index), 0)[1], 0)

        lax.fori_loop(begin(step), begin(step + 1), lambda unit, _: (expert_unit(unit), 0)[1], 0)
        return 0

    lax.fori_loop(0, rounds + 2, step_body, 0)

    def row_store(index):
        rows = pl.ds(pl.multiple_of(index * tile, tile), tile)
        slot = remainder(index, 4)
        return pltpu.make_async_copy(row_buf.at[slot], out_ref.at[rows, :], row_sem.at[slot])

    def store_tile(index, _):
        @pl.when(index >= 4)
        def _():
            row_store(index - 4).wait()
        rows = pl.ds(pl.multiple_of(index * tile, tile), tile)
        row_buf[remainder(index, 4)] = total[rows, :].astype(row_buf.dtype)
        row_store(index).start()
        return 0

    lax.fori_loop(0, 8, store_tile, 0)
    for index in range(4, 8):
        row_store(index).wait()

    def finish(index, _):
        for flow in range(2):
            wait_send(ring_copy(flow, index, False))
            wait_send(side_copy(flow, index, parity))
        for flow in range(4):
            wait_send(pair_copy(flow, index, core))
        return 0

    lax.fori_loop(0, rounds, finish, 0)
    wait_send(own_copy(ep))


def solution(mesh):
    group_size = mesh.shape["ep"]
    columns = math.isqrt(mesh.shape["dp"])
    rows_spec = P(("dp", "ep"))

    def device_step(hidden, ln_gamma, ln_beta, w_router, w_gate, w_up, w_down, choice, mask_first, mask_second):
        tokens, width = hidden.shape
        experts = w_gate.shape[0] * group_size
        ff = w_gate.shape[2]
        capacity = (10 * tokens + 4 * experts - 1) // (4 * experts)
        ring = group_size // 2
        rounds = SPLIT * (ring - 1)
        padded = -(-ff // LANES) * LANES
        own = jnp.stack([w_gate[0].T, w_up[0].T, w_down[0]])
        dma = pltpu.SemaphoreType.DMA
        whole = pl.BlockSpec(memory_space=pl.ANY)
        local = pl.BlockSpec(memory_space=pltpu.VMEM)
        out, _ = pl.pallas_call(
            functools.partial(moe_kernel, (ring, columns, capacity)),
            out_shape=(jax.ShapeDtypeStruct(hidden.shape, hidden.dtype),
                       jax.ShapeDtypeStruct((experts, 3, ff, width), w_down.dtype)),
            in_specs=[whole, local, local, local, whole, local, local, local],
            out_specs=(whole, whole),
            scratch_shapes=[
                pltpu.VMEM((tokens, width), jnp.bfloat16),
                pltpu.VMEM((tokens, width), jnp.float32),
                pltpu.VMEM((2, 2 * ff, width), w_gate.dtype),
                pltpu.VMEM((2, padded, width), w_down.dtype),
                pltpu.VMEM((4, tokens // 8, width), hidden.dtype),
                pltpu.VMEM((tokens // 2, padded), jnp.bfloat16),
                pltpu.VMEM((tokens, experts), jnp.float32),
                pltpu.VMEM((tokens // 2, LANES), jnp.float32),
                dma((2, rounds)), dma((2, rounds)),
                dma((2, rounds)), dma((2, rounds)),
                dma((4, rounds)), dma((4, rounds)),
                dma((1,)), dma((1,)),
                dma((4,)), dma((2, 1 + 2 * (padded // LANES))),
            ],
            compiler_params=pltpu.CompilerParams(collective_id=0, has_side_effects=True, vmem_limit_bytes=67043328),
            name="moe",
        )(hidden, ln_gamma.reshape(1, width), ln_beta.reshape(1, width), w_router.T, own,
          choice.T, mask_first.T, mask_second.T)
        return out

    return jax.shard_map(device_step, mesh=mesh,
                         in_specs=(rows_spec, P(), P(), P(), P("ep"), P("ep"), P("ep"), rows_spec, rows_spec, rows_spec),
                         out_specs=rows_spec, check_vma=False)
```

time: 584 us -> 556 us (0.952)
  local copies, waits for them, and re-layouts: 49 us -> 7.89 us
  other arithmetic: 0 us -> 9.65 us
  Pallas kernels: 533 us -> 539 us
    unnamed x7 -> x1, local copies, waits for them, and re-layouts: 28.3 us -> 7.89 us
    concatenate x1 -> x0, local copies, waits for them, and re-layouts: 11.4 us -> none  [pack_gate_up(): return jnp.concatenate(pieces, axis=1)]
    another operation x0 -> x1, other arithmetic: none -> 9.65 us  [device_step(): own = jnp.stack([w_gate[0].T, w_up[0].T, w_down[0]])]
    slice x3 -> x0, local copies, waits for them, and re-layouts: 9.3 us -> none  [pack_gate_up(): pieces += [w_gate[:, low:high], w_up[:, low:high]]]
where the time goes in v2:
time: 556 us
  Pallas kernels  539 us (97%)
  other arithmetic  9.65 us (2%)
  local copies, waits for them, and re-layouts  7.89 us (1%)
    pallas_call x1, Pallas kernels, device_step(): pl.pallas_call(functools.partial(moe_kernel, (ring, columns, capacity)),...  539 us

profile of v2, /device:TPU:22, one launch (start us, length us, event | category | flops | bytes accessed | tf_op | source)
XLA Modules:
  0.0 556.1 jit_solution(2542012599820581698)
XLA Ops:
  0.0 9.6 %pad_maximum_fusion.own_ref = bf16[3,448,4096]{2,1,0:T(8,128)(2,1)} fusion(bf16[1,448,4096]{2,1,0:T(8,128)(2,1)} %param.16, bf16[1,448,4096]{2,1,0:T(8,128)(2,1)} %bitcast.16, bf16[1,448,4096]{2,1,0:T(8,128)(2,1)} %bitcast.17), kind=kLoop, calls=%fused_computation | loop fusion | flops 11010048 | bytes 22020096 | tf_op jit(solution)/shard_map/stack | solution.py:329
  9.6 538.6 %moe.1 = (bf16[1024,4096]{1,0:T(8,128)(2,1)}, bf16[16,3,448,4096]{3,2,1,0:T(8,128)(2,1)}) custom-call(bf16[1024,4096]{1,0:T(8,128)(2,1)} %hidden_ref.1, f32[1,4096]{1,0:T(1,128)} %bitcast.21, f32[1,4096]{1,0:T(1,128)} %bitcast.22, bf16[16,4096]{1,0:T(8,128)(2,1)} %bitcast.18, bf16[3,448,4096]{2,1,0:T(8,128)(2,1)} %pad_maximum_fusion.own_ref, ...), custom_call_target="tpu_custom_call" | custom-call | tf_op jit(solution)/shard_map/moe/pallas_call | solution.py:333
  548.3 7.9 %copy.12 = bf16[1024,4096]{1,0:T(8,128)(2,1)} copy(bf16[1024,4096]{1,0:T(8,128)(2,1)} %get-tuple-element.6) | data formatting | bytes 16777216
